TPU v7x, 32 devices: a whole 2x2x4 slice. The times are simulated.
32 devices in a mesh: row: 16 (over z, y, x), col: 2 (over core).
Axes of the slice: x: 2, y: 2, z: 4, core: 2. Of those that a mesh axis runs over, the one named last changes fastest.
Arguments:
- sources: bfloat16 [32768, 640], P(('row', 'col')), may hold values from -6 to 6
- tree_perm: int32 [32768], P(('row', 'col')), may hold values from 0 to 32767, as said below
- leaf_blocks: bfloat16 [32768, 512], P(('row', 'col')), may hold values from -0.25 to 0.25
- u_factors: bfloat16 [6, 32, 32768], P(None, None, ('row', 'col')), may hold values from -0.4375 to 0.4375
- v_factors: bfloat16 [6, 32, 32768], P(None, None, ('row', 'col')), as said below
- level_ranks: int32 [6], replicated, may hold values from 16 to 32
Outputs:
- products: bfloat16 [32768, 640], P(('row', 'col'))
Inputs may be any that keep to these rules, and one draw needn't show every extreme that they name: tree_perm is a permutation that maps each aligned block of 1024 positions onto the same block of initial indices. `v_factors`: entries of level l are of the order of the inverse square root of 32768 / 2^l.
All inputs are finite; a program needn't handle non-finite values.
Results may differ from a plain program's by a relative error of at most 0.0037.
Values sent between devices are 32-bit elements; how exact they have to be, the bound alone decides.
A program may use at most 64 MiB of HBM per device.

v0:
```python
import jax
import jax.numpy as jnp
from jax import lax
from jax.sharding import PartitionSpec as P


def partner(x, axis, distance):
    return lax.ppermute(x, axis, [(i, i ^ 1 << distance) for i in range(lax.axis_size(axis))])


def per_device(sources, tree_perm, leaf_blocks, u_factors, v_factors, level_ranks):
    row_count, rhs_count = sources.shape
    leaf_size = leaf_blocks.shape[1]
    level_count, rank_cap, _ = u_factors.shape
    col_size = lax.axis_size("col")
    col_bits = col_size.bit_length() - 1
    row_bits = lax.axis_size("row").bit_length() - 1
    dev_bits = row_bits + col_bits
    first_row = (lax.axis_index("row") * col_size + lax.axis_index("col")) * row_count
    local_index = tree_perm - first_row
    ordered = sources[local_index]
    rank_mask = (lax.iota(jnp.int32, rank_cap)[None, :] < level_ranks[:, None]).astype(jnp.float32)
    partial_coef = jnp.einsum(
        "lkn,nr->lkr", v_factors[:dev_bits], ordered, preferred_element_type=jnp.float32
    )
    siblings = [None] * dev_bits
    running = partial_coef
    for bit_pos in range(col_bits):
        finish = dev_bits - 1 - bit_pos
        received = partner(running, "col", bit_pos)
        siblings[finish] = received[finish]
        running = running[:finish] + received[:finish]
    share_width = rhs_count // col_size
    running = lax.dynamic_slice_in_dim(running, lax.axis_index("col") * share_width, share_width, 2)
    coarse = [None] * row_bits
    for level in range(row_bits):
        level_sum = running[level]
        for bit_pos in range(row_bits - 1 - level):
            level_sum = level_sum + partner(level_sum, "row", bit_pos)
        coarse[level] = partner(level_sum, "row", row_bits - 1 - level)
    coarse_stack = jnp.stack(coarse)
    coarse_stack = lax.all_gather(coarse_stack, "col", axis=2, tiled=True)
    far_coef = (
        jnp.concatenate([coarse_stack, jnp.stack(siblings[row_bits:])], axis=0)
        * rank_mask[:dev_bits, :, None]
    ).astype(jnp.bfloat16)
    leaf_count = row_count // leaf_size
    result = jnp.einsum(
        "gij,gjr->gir",
        leaf_blocks.reshape(leaf_count, leaf_size, leaf_size),
        ordered.reshape(leaf_count, leaf_size, rhs_count),
        preferred_element_type=jnp.float32,
    ).reshape(row_count, rhs_count)
    result = result + jnp.einsum(
        "lkn,lkr->nr", u_factors[:dev_bits], far_coef, preferred_element_type=jnp.float32
    )
    for level in range(dev_bits, level_count):
        cluster_rows = row_count >> level - dev_bits + 1
        groups = row_count // cluster_rows
        near_coef = jnp.einsum(
            "kgs,gsr->gkr",
            v_factors[level].reshape(rank_cap, groups, cluster_rows),
            ordered.reshape(groups, cluster_rows, rhs_count),
            preferred_element_type=jnp.float32,
        )
        near_coef = near_coef.reshape(groups // 2, 2, rank_cap, rhs_count)[:, ::-1].reshape(
            groups, rank_cap, rhs_count
        )
        near_coef = (near_coef * rank_mask[level][None, :, None]).astype(jnp.bfloat16)
        result = result + jnp.einsum(
            "kgs,gkr->gsr",
            u_factors[level].reshape(rank_cap, groups, cluster_rows),
            near_coef,
            preferred_element_type=jnp.float32,
        ).reshape(row_count, rhs_count)
    return jnp.zeros_like(sources).at[local_index].set(result.astype(jnp.bfloat16))


def solution(mesh):
    placed = (
        P(("row", "col"), None),
        P(("row", "col")),
        P(("row", "col"), None),
        P(None, None, ("row", "col")),
        P(None, None, ("row", "col")),
        P(),
    )
    return jax.shard_map(
        per_device, mesh=mesh, in_specs=placed, out_specs=P(("row", "col"), None), check_vma=False
    )
```

profile of v0, /device:TPU:0, one launch (start us, length us, event | category | flops | bytes accessed | tf_op | source)
XLA Modules:
  0.0 56.9 jit_solution(1084728093172403832)
XLA Ops:
  0.0 0.0 copy-start
  0.0 0.8 %broadcast_clamp_fusion = (s32[1024]{0:T(1024)S(1)}, s32[1024]{0:T(1024)S(1)}) fusion(s32[1024]{0:T(1024)} %param.7, s32[]{:T(128)S(6)} %mul.28), kind=kLoop, calls=%fused_computation.29 | loop fusion | flops 5120 | bytes 12292 | tf_op jit(solution)/shard_map/gather | solution.py:21
  0.8 0.5 copy-done
  1.3 0.0 copy-start.3
  1.3 4.0 %gather_fusion = bf16[1024,640]{1,0:T(8,128)(2,1)S(1)} fusion(bf16[1024,640]{1,0:T(8,128)(2,1)S(1)} %copy-done, s32[1024]{0:T(1024)S(1)} %get-tuple-element.5), kind=kCustom, calls=%fused_computation | custom fusion | bytes 2625536 | tf_op jit(solution)/shard_map/gather | solution.py:21
  5.4 0.0 copy-done.3
  5.4 1.2 %fusion.4 = f32[5,32,640]{2,1,0:T(8,128)} fusion(bf16[1024,640]{1,0:T(8,128)(2,1)S(1)} %gather_fusion, bf16[6,32,1024]{2,1,0:T(8,128)(2,1)S(1)} %copy-done.3), kind=kOutput, calls=%fused_computation.7 | convolution fusion | flops 209715200 | bytes 2048000 | tf_op jit(solution)/shard_map/lkn,nr->lkr/dot_general | solution.py:23
  6.6 0.5 collective-permute-start
  7.1 0.8 %slice.49 = bf16[1,32,1024]{2,1,0:T(8,128)(2,1)S(1)} slice(bf16[6,32,1024]{2,1,0:T(8,128)(2,1)} %param.10), slice={[5:6], [0:32], [0:1024]} | slice | bytes 131072 | tf_op jit(solution)/shard_map/slice | solution.py:62
  7.9 0.3 convolution_bitcast_fusion
  8.3 1.0 %slice.54 = f32[4,32,640]{2,1,0:T(8,128)S(1)} slice(f32[5,32,640]{2,1,0:T(8,128)} %fusion.4), slice={[0:4], [0:32], [0:640]} | slice | bytes 655360 | tf_op jit(solution)/shard_map/slice | solution.py:32
  9.3 3.7 %fusion.22 = f32[2,640,512]{1,2,0:T(8,128)} fusion(bf16[2,512,512]{2,1,0:T(8,128)(2,1)} %bitcast.55, bf16[2,512,640]{2,1,0:T(8,128)(2,1)S(1)} %bitcast.52), kind=kOutput, calls=%fused_computation.35 | convolution fusion | flops 671088640 | bytes 4980736 | tf_op jit(solution)/shard_map/gij,gjr->gir/dot_general | solution.py:48
  13.0 0.0 copy-start.4
  13.0 0.0 slice-start.1
  13.0 0.0 collective-permute-done
  13.0 0.0 copy-start.1
  13.0 0.2 dynamic-slice_add_fusion
  13.2 2.5 %collective-permute-start.1 = (f32[32,320]{1,0:T(8,128)S(1)}, f32[32,320]{1,0:T(8,128)S(1)}, u32[]{:S(2)}, u32[]{:S(2)}) collective-permute-start(f32[32,320]{1,0:T(8,128)S(1)} %get-tuple-element.10), channel_id=1, source_target_pairs={{0,2},{2,0},{4,6},{6,4},{8,10},{10,8},{12,14},{14,12},{16,18},{18,... | collective-permute-start | bytes 122888 | tf_op jit(solution)/shard_map/ppermute | solution.py:8
  15.8 0.1 collective-permute-start.8
  15.9 1.9 %collective-permute-start.5 = (f32[32,320]{1,0:T(8,128)S(1)}, f32[32,320]{1,0:T(8,128)S(1)}, u32[]{:S(2)}, u32[]{:S(2)}) collective-permute-start(f32[32,320]{1,0:T(8,128)S(1)} %get-tuple-element.12), channel_id=1, source_target_pairs={{0,2},{2,0},{4,6},{6,4},{8,10},{10,8},{12,14},{14,12},{16,18},{18,... | collective-permute-start | bytes 122888 | tf_op jit(solution)/shard_map/ppermute | solution.py:8
  17.8 0.0 copy-done.4
  17.8 0.1 fusion.17
  17.9 0.3 collective-permute-done.1
  18.2 2.0 %collective-permute-done.8 = f32[32,320]{1,0:T(8,128)S(1)} collective-permute-done((f32[32,320]{1,0:T(8,128)S(1)}, f32[32,320]{1,0:T(8,128)S(1)}, u32[]{:S(2)}, u32[]{:S(2)}) %collective-permute-start.8) | collective-permute-done | bytes 40992 | tf_op jit(solution)/shard_map/ppermute | solution.py:8
  20.2 0.5 collective-permute-done.5
  20.7 1.6 %collective-permute-start.2 = (f32[32,320]{1,0:T(8,128)S(1)}, f32[32,320]{1,0:T(8,128)S(1)}, u32[]{:S(2)}, u32[]{:S(2)}) collective-permute-start(f32[32,320]{1,0:T(8,128)S(1)} %get-tuple-element.7), channel_id=1, source_target_pairs={{0,4},{2,6},{4,0},{6,2},{8,12},{10,14},{12,8},{14,10},{16,20},{18,... | collective-permute-start | bytes 122888 | tf_op jit(solution)/shard_map/ppermute | solution.py:8
  22.3 0.5 collective-permute-start.6
  22.8 2.2 %collective-permute-done.2 = f32[32,320]{1,0:T(8,128)S(1)} collective-permute-done((f32[32,320]{1,0:T(8,128)S(1)}, f32[32,320]{1,0:T(8,128)S(1)}, u32[]{:S(2)}, u32[]{:S(2)}) %collective-permute-start.2) | collective-permute-done | bytes 40992 | tf_op jit(solution)/shard_map/ppermute | solution.py:8
  25.1 1.6 %collective-permute-start.3 = (f32[32,320]{1,0:T(8,128)S(1)}, f32[32,320]{1,0:T(8,128)S(1)}, u32[]{:S(2)}, u32[]{:S(2)}) collective-permute-start(f32[32,320]{1,0:T(8,128)S(1)} %add.42), channel_id=1, source_target_pairs={{0,8},{2,10},{4,12},{6,14},{8,0},{10,2},{12,4},{14,6},{16,24},{18,... | collective-permute-start | bytes 122888 | tf_op jit(solution)/shard_map/ppermute | solution.py:8
  26.7 0.1 multiply_convert_fusion
  26.8 0.0 slice-done.1
  26.9 1.7 %collective-permute-start.10 = (f32[32,320]{1,0:T(8,128)S(1)}, f32[32,320]{1,0:T(8,128)S(1)}, u32[]{:S(2)}, u32[]{:S(2)}) collective-permute-start(f32[32,320]{1,0:T(8,128)S(1)} %get-tuple-element.13), channel_id=1, source_target_pairs={{0,2},{2,0},{4,6},{6,4},{8,10},{10,8},{12,14},{14,12},{16,18},{18,... | collective-permute-start | bytes 122888 | tf_op jit(solution)/shard_map/ppermute | solution.py:8
  28.5 1.1 %collective-permute-start.9 = (f32[32,320]{1,0:T(8,128)S(1)}, f32[32,320]{1,0:T(8,128)S(1)}, u32[]{:S(2)}, u32[]{:S(2)}) collective-permute-start(f32[32,320]{1,0:T(8,128)S(1)} %get-tuple-element.8), channel_id=1, source_target_pairs={{0,4},{2,6},{4,0},{6,2},{8,12},{10,14},{12,8},{14,10},{16,20},{18,... | collective-permute-start | bytes 122888 | tf_op jit(solution)/shard_map/ppermute | solution.py:8
  29.6 0.0 collective-permute-done.6
  29.6 0.5 collective-permute-start.7
  30.1 0.0 collective-permute-done.3
  30.1 2.7 %collective-permute-start.4 = (f32[32,320]{1,0:T(8,128)S(1)}, f32[32,320]{1,0:T(8,128)S(1)}, u32[]{:S(2)}, u32[]{:S(2)}) collective-permute-start(f32[32,320]{1,0:T(8,128)S(1)} %add.43), channel_id=1, source_target_pairs={{0,16},{2,18},{4,20},{6,22},{8,24},{10,26},{12,28},{14,30},{16,0},... | collective-permute-start | bytes 122888 | tf_op jit(solution)/shard_map/ppermute | solution.py:8
  32.8 2.0 %fusion.14 = f32[2,640,512]{1,2,0:T(8,128)} fusion(bf16[2,32,640]{2,1,0:T(8,128)(2,1)S(1)} %multiply_convert_fusion, bf16[32,2,512]{2,1,0:T(2,128)(2,1)S(1)} %reshape_squeeze.7), kind=kOutput, calls=%fused_computation.19 | convolution fusion | flops 41943040 | bytes 2768896 | tf_op jit(solution)/shard_map/kgs,gkr->gsr/dot_general | solution.py:70
  34.8 3.3 %copy.35 = f32[1024,640]{0,1:T(8,128)} copy(f32[1024,640]{1,0:T(8,128)} %bitcast.54) | data formatting | bytes 5242880 | tf_op jit(solution)/shard_map/reshape | solution.py:75
  38.1 3.3 %copy.30 = f32[1024,640]{0,1:T(8,128)} copy(f32[1024,640]{1,0:T(8,128)} %bitcast.53) | data formatting | bytes 5242880 | tf_op jit(solution)/shard_map/reshape | solution.py:53
  41.4 0.0 copy-done.1
  41.4 0.0 collective-permute-done.10
  41.4 0.0 collective-permute-done.9
  41.4 0.0 collective-permute-done.7
  41.4 0.0 collective-permute-done.4
  41.4 0.3 copy.28
  41.7 2.7 %all_gather.3 = f32[4,32,640]{1,0,2:T(4,128)S(1)} all-gather(f32[4,32,320]{1,0,2:T(4,128)S(1)} %copy.28), channel_id=1, replica_groups=mesh['row'=16,'col'=2] {'col'}, dimensions={2}, use_global_device_ids=true | all-gather | bytes 491520 | tf_op jit(solution)/shard_map/all_gather | solution.py:42
  44.4 0.0 slice-start
  44.4 0.0 copy-start.2
  44.4 0.4 copy.29
  44.8 0.5 slice-done
  45.3 0.2 copy-done.2
  45.5 3.1 %fusion.1 = bf16[1024,640]{0,1:T(8,128)(2,1)S(1)} fusion(f32[1024,640]{0,1:T(8,128)} %copy.35, f32[1024,640]{0,1:T(8,128)} %copy.30, bf16[6,32,1024]{2,1,0:T(8,128)(2,1)S(1)} %copy-done.2, f32[1,32,640]{2,1,0:T(8,128)S(1)} %slice-done, f32[4,32,640]{2,1,0:T(8,128)S(1)} %copy.29, f32[5,32]{1,0:T(8,128)S(1)} %bitcast.60), kind=kOutput, calls=%fused_computation.4 | convolution fusion | flops 211988480 | bytes 7294976 | tf_op jit(solution)/shard_map/lkn,lkr->nr/dot_general | solution.py:54
  48.6 1.5 %copy.34 = bf16[1024,640]{1,0:T(8,128)(2,1)} copy(bf16[1024,640]{0,1:T(8,128)(2,1)S(1)} %fusion.1) | data formatting | bytes 2621440 | tf_op jit(solution)/shard_map/convert_element_type | solution.py:76
  50.1 6.8 %scatter_custom_fusion = bf16[1024,640]{1,0:T(8,128)(2,1)} fusion(s32[1024]{0:T(1024)S(1)} %get-tuple-element.6, bf16[1024,640]{1,0:T(8,128)(2,1)} %copy.34, bf16[]{:T(256)} %constant.8.clone.1), kind=kCustom, calls=%fused_computation.9 | custom fusion | bytes 1311232 | tf_op jit(solution)/shard_map/scatter | solution.py:76
  (10 shorter events, 0.2 us)
Async XLA Ops:
  0.0 1.3 %copy-start = (bf16[1024,640]{1,0:T(8,128)(2,1)S(1)}, bf16[1024,640]{1,0:T(8,128)(2,1)}, u32[]{:S(2)}) copy-start(bf16[1024,640]{1,0:T(8,128)(2,1)} %param.6) | copy-start | bytes 3932164
  1.3 4.0 %copy-start.3 = (bf16[6,32,1024]{2,1,0:T(8,128)(2,1)S(1)}, bf16[6,32,1024]{2,1,0:T(8,128)(2,1)}, u32[]{:S(2)}) copy-start(bf16[6,32,1024]{2,1,0:T(8,128)(2,1)} %param.10) | copy-start | bytes 1179652
  6.6 6.4 %collective-permute-start = (f32[5,32,640]{2,1,0:T(8,128)}, f32[5,32,640]{2,1,0:T(8,128)S(1)}, u32[]{:S(2)}, u32[]{:S(2)}) collective-permute-start(f32[5,32,640]{2,1,0:T(8,128)} %fusion.4), channel_id=1, source_target_pairs={{0,1},{1,0},{2,3},{3,2},{4,5},{5,4},{6,7},{7,6},{8,9},{9,8},{10,11... | collective-permute-start | bytes 1228808 | tf_op jit(solution)/shard_map/ppermute | solution.py:8
  13.0 4.8 %copy-start.4 = (s32[6]{0:T(128)S(1)}, s32[6]{0:T(128)}, u32[]{:S(2)}) copy-start(s32[6]{0:T(128)} %param.11) | copy-start | bytes 76
  13.0 13.8 %slice-start.1 = ((bf16[6,32,1024]{2,1,0:T(8,128)(2,1)}), bf16[1,32,1024]{2,1,0:T(8,128)(2,1)S(1)}, s32[]{:S(2)}) async-start(bf16[6,32,1024]{2,1,0:T(8,128)(2,1)} %param.9), calls=%async_computation.1 | async-start | bytes 131072 | tf_op jit(solution)/shard_map/slice | solution.py:72
  13.0 28.4 %copy-start.1 = (f32[5,32,640]{2,1,0:T(8,128)}, f32[5,32,640]{2,1,0:T(8,128)S(1)}, u32[]{:S(2)}) copy-start(f32[5,32,640]{2,1,0:T(8,128)S(1)} %collective-permute-done) | copy-start | bytes 1228804
  13.2 5.0 %collective-permute-start.1 = (f32[32,320]{1,0:T(8,128)S(1)}, f32[32,320]{1,0:T(8,128)S(1)}, u32[]{:S(2)}, u32[]{:S(2)}) collective-permute-start(f32[32,320]{1,0:T(8,128)S(1)} %get-tuple-element.10), channel_id=1, source_target_pairs={{0,2},{2,0},{4,6},{6,4},{8,10},{10,8},{12,14},{14,12},{16,18},{18,... | collective-permute-start | bytes 122888 | tf_op jit(solution)/shard_map/ppermute | solution.py:8
  15.8 4.4 %collective-permute-start.8 = (f32[32,320]{1,0:T(8,128)S(1)}, f32[32,320]{1,0:T(8,128)S(1)}, u32[]{:S(2)}, u32[]{:S(2)}) collective-permute-start(f32[32,320]{1,0:T(8,128)S(1)} %get-tuple-element.11), channel_id=1, source_target_pairs={{0,2},{2,0},{4,6},{6,4},{8,10},{10,8},{12,14},{14,12},{16,18},{18,... | collective-permute-start | bytes 122888 | tf_op jit(solution)/shard_map/ppermute | solution.py:8
  15.9 4.8 %collective-permute-start.5 = (f32[32,320]{1,0:T(8,128)S(1)}, f32[32,320]{1,0:T(8,128)S(1)}, u32[]{:S(2)}, u32[]{:S(2)}) collective-permute-start(f32[32,320]{1,0:T(8,128)S(1)} %get-tuple-element.12), channel_id=1, source_target_pairs={{0,2},{2,0},{4,6},{6,4},{8,10},{10,8},{12,14},{14,12},{16,18},{18,... | collective-permute-start | bytes 122888 | tf_op jit(solution)/shard_map/ppermute | solution.py:8
  20.7 4.3 %collective-permute-start.2 = (f32[32,320]{1,0:T(8,128)S(1)}, f32[32,320]{1,0:T(8,128)S(1)}, u32[]{:S(2)}, u32[]{:S(2)}) collective-permute-start(f32[32,320]{1,0:T(8,128)S(1)} %get-tuple-element.7), channel_id=1, source_target_pairs={{0,4},{2,6},{4,0},{6,2},{8,12},{10,14},{12,8},{14,10},{16,20},{18,... | collective-permute-start | bytes 122888 | tf_op jit(solution)/shard_map/ppermute | solution.py:8
  22.3 7.3 %collective-permute-start.6 = (f32[32,320]{1,0:T(8,128)S(1)}, f32[32,320]{1,0:T(8,128)S(1)}, u32[]{:S(2)}, u32[]{:S(2)}) collective-permute-start(f32[32,320]{1,0:T(8,128)S(1)} %get-tuple-element.9), channel_id=1, source_target_pairs={{0,4},{2,6},{4,0},{6,2},{8,12},{10,14},{12,8},{14,10},{16,20},{18,... | collective-permute-start | bytes 122888 | tf_op jit(solution)/shard_map/ppermute | solution.py:8
  25.1 5.1 %collective-permute-start.3 = (f32[32,320]{1,0:T(8,128)S(1)}, f32[32,320]{1,0:T(8,128)S(1)}, u32[]{:S(2)}, u32[]{:S(2)}) collective-permute-start(f32[32,320]{1,0:T(8,128)S(1)} %add.42), channel_id=1, source_target_pairs={{0,8},{2,10},{4,12},{6,14},{8,0},{10,2},{12,4},{14,6},{16,24},{18,... | collective-permute-start | bytes 122888 | tf_op jit(solution)/shard_map/ppermute | solution.py:8
  26.9 14.5 %collective-permute-start.10 = (f32[32,320]{1,0:T(8,128)S(1)}, f32[32,320]{1,0:T(8,128)S(1)}, u32[]{:S(2)}, u32[]{:S(2)}) collective-permute-start(f32[32,320]{1,0:T(8,128)S(1)} %get-tuple-element.13), channel_id=1, source_target_pairs={{0,2},{2,0},{4,6},{6,4},{8,10},{10,8},{12,14},{14,12},{16,18},{18,... | collective-permute-start | bytes 122888 | tf_op jit(solution)/shard_map/ppermute | solution.py:8
  28.5 12.8 %collective-permute-start.9 = (f32[32,320]{1,0:T(8,128)S(1)}, f32[32,320]{1,0:T(8,128)S(1)}, u32[]{:S(2)}, u32[]{:S(2)}) collective-permute-start(f32[32,320]{1,0:T(8,128)S(1)} %get-tuple-element.8), channel_id=1, source_target_pairs={{0,4},{2,6},{4,0},{6,2},{8,12},{10,14},{12,8},{14,10},{16,20},{18,... | collective-permute-start | bytes 122888 | tf_op jit(solution)/shard_map/ppermute | solution.py:8
  29.6 11.8 %collective-permute-start.7 = (f32[32,320]{1,0:T(8,128)S(1)}, f32[32,320]{1,0:T(8,128)S(1)}, u32[]{:S(2)}, u32[]{:S(2)}) collective-permute-start(f32[32,320]{1,0:T(8,128)S(1)} %add.45), channel_id=1, source_target_pairs={{0,8},{2,10},{4,12},{6,14},{8,0},{10,2},{12,4},{14,6},{16,24},{18,... | collective-permute-start | bytes 122888 | tf_op jit(solution)/shard_map/ppermute | solution.py:8
  30.1 11.2 %collective-permute-start.4 = (f32[32,320]{1,0:T(8,128)S(1)}, f32[32,320]{1,0:T(8,128)S(1)}, u32[]{:S(2)}, u32[]{:S(2)}) collective-permute-start(f32[32,320]{1,0:T(8,128)S(1)} %add.43), channel_id=1, source_target_pairs={{0,16},{2,18},{4,20},{6,22},{8,24},{10,26},{12,28},{14,30},{16,0},... | collective-permute-start | bytes 122888 | tf_op jit(solution)/shard_map/ppermute | solution.py:8
  44.4 0.9 %slice-start = ((f32[5,32,640]{2,1,0:T(8,128)}), f32[1,32,640]{2,1,0:T(8,128)S(1)}, s32[]{:S(2)}) async-start(f32[5,32,640]{2,1,0:T(8,128)} %copy-done.1), calls=%async_computation | async-start | bytes 163840 | tf_op jit(solution)/shard_map/slice | solution.py:31
  44.4 1.0 %copy-start.2 = (bf16[6,32,1024]{2,1,0:T(8,128)(2,1)S(1)}, bf16[6,32,1024]{2,1,0:T(8,128)(2,1)}, u32[]{:S(2)}) copy-start(bf16[6,32,1024]{2,1,0:T(8,128)(2,1)} %param.9) | copy-start | bytes 1179652
where the time goes:
time: 57.3 us; the launch traced here: 56.9 us
  local copies, waits for them, and re-layouts  22.6 us (39%)
  starting transfers between devices  14.7 us (26%)
  matrix products  10.4 us (18%)
  waiting for transfers between devices  5.07 us (9%)
  blocking collectives  2.74 us (5%)
  other arithmetic  1.2 us (2%)
    ppermute x11, starting transfers between devices, partner(): lax.ppermute(x, axis, [(i, i ^ 1 << distance) for i in range(lax.axis_siz...  14.7 us
    scatter x1, local copies, waits for them, and re-layouts, per_device(): jnp.zeros_like(sources).at[local_index].set(result.astype(jnp.bfloat16))  6.79 us
    ppermute x11, waiting for transfers between devices, partner(): lax.ppermute(x, axis, [(i, i ^ 1 << distance) for i in range(lax.axis_siz...  5.07 us
    gather x1, local copies, waits for them, and re-layouts, per_device(): ordered = sources[local_index]  4.02 us
    dot_general x1, matrix products, per_device(): jnp.einsum('gij,gjr->gir', leaf_blocks.reshape(leaf_count, leaf_size, lea...  3.71 us
    reshape x1, local copies, waits for them, and re-layouts, per_device(): result = result + jnp.einsum('kgs,gkr->gsr', u_factors[level].reshape(ran...  3.28 us
    reshape x1, local copies, waits for them, and re-layouts, per_device(): result = jnp.einsum('gij,gjr->gir', leaf_blocks.reshape(leaf_count, leaf_...  3.25 us
    dot_general x1, matrix products, per_device(): jnp.einsum('lkn,lkr->nr', u_factors[:dev_bits], far_coef, preferred_eleme...  3.14 us
  transfers between devices with their start and end apart: 11, of which 4 were waited for; matrix products, arithmetic and copies ran while one was open for 26% of the time, Pallas kernels for 0%

commit v1 on v0

v1 whole, which is shorter than its diff:
```python
import functools

import jax
import jax.numpy as jnp
from jax import lax
from jax.experimental import pallas as pl
from jax.experimental.pallas import tpu as pltpu
from jax.sharding import PartitionSpec as P

F32 = jnp.float32
BF16 = jnp.bfloat16


def flip(x, mask):
    bit = 0
    while mask >> bit:
        if mask >> bit & 1:
            x = x + (1 << bit) * (1 - 2 * lax.rem(lax.div(x, 1 << bit), 2))
        bit += 1
    return x


def split_bits(dev_bits):
    groups, start = [], 0
    while start < dev_bits:
        bits = min(3, dev_bits - start)
        groups.append((start, bits))
        start += bits
    return groups


def top_bit(k):
    return k.bit_length() - 1


def kernel(
    cfg,
    ranks_ref, perm_ref, src_hbm, leaf_hbm, u_hbm, v_hbm,
    out_hbm,
    src, leaf, u, v, one_hot, one_hot_t, ordered, mixed, u_perm, u_near, near, acc, far, staged,
    *rest,
):
    rows, rhs, leaf_size, levels, rank, row_size, col_size, groups = cfg
    dev_bits = sum(bits for _, bits in groups)
    base_bits = groups[0][1]
    base = 1 << base_bits
    upper = dev_bits - base_bits
    part = rank // base
    rest = list(rest)
    low_send = [rest.pop(0) for _ in range(base_bits)]
    low_recv = [rest.pop(0) for _ in range(base_bits)]
    low_full = [rest.pop(0) for _ in range(base_bits)]
    up_send, up_recv, up_full = [rest.pop(0) for _ in range(3)]
    hold = [rest.pop(0) for _ in groups[1:]]
    recv_own = [rest.pop(0) for _ in groups[1:]]
    recv_above = [rest.pop(0) for _ in groups[1:]]
    in_sem, out_sem, send_sem, recv_sem = rest

    me = lax.axis_index("row") * col_size + lax.axis_index("col")
    mine = lax.rem(me, base)

    loads = []
    half = rows // 2
    for at, (a, b) in enumerate(
        [(v_hbm, v)]
        + [(src_hbm.at[pl.ds(h * half, half)], src.at[pl.ds(h * half, half)]) for h in range(2)]
        + [(u_hbm, u), (leaf_hbm, leaf)]
    ):
        copy = pltpu.make_async_copy(a, b, in_sem.at[at])
        copy.start()
        loads.append(copy)

    barrier = pltpu.get_barrier_semaphore()
    partners = [k << start for start, bits in groups for k in range(1, 1 << bits)]

    def device(mask):
        other = flip(me, mask)
        return (lax.div(other, col_size), lax.rem(other, col_size))

    for mask in partners:
        pl.semaphore_signal(
            barrier, inc=1, device_id=device(mask), device_id_type=pl.DeviceIdType.MESH
        )

    count = [0]
    copies = []

    def send(source, target, mask):
        at = count[0]
        count[0] += 1
        copy = pltpu.make_async_remote_copy(
            src_ref=source,
            dst_ref=target,
            send_sem=send_sem.at[at],
            recv_sem=recv_sem.at[at],
            device_id=device(mask),
            device_id_type=pl.DeviceIdType.MESH,
        )
        copy.start()
        copies.append(copy)
        return copy

    local = (perm_ref[...] - me * rows).astype(F32)
    wide = jnp.broadcast_to(local, (128, rows)).T
    lane = lax.broadcasted_iota(jnp.int32, (rows, 128), 1).astype(F32)
    for c in range(rows // 128):
        one_hot[:, c * 128:(c + 1) * 128] = jnp.where(wide == lane + c * 128.0, 1.0, 0.0).astype(BF16)

    loads[0].wait()
    v_all = v[...].reshape(levels * rank, rows)
    v_perm = jnp.dot(v_all[: dev_bits * rank], one_hot[...], preferred_element_type=F32).astype(BF16)
    loads[1].wait()
    loads[2].wait()
    coef = jnp.dot(v_perm, src[...], preferred_element_type=F32)
    staged[...] = coef
    for p in range(base_bits, dev_bits):
        first = (dev_bits - 1 - p) * rank
        for q in range(base):
            up_send[q, p - base_bits] = staged[first + q * part:first + (q + 1) * part]

    pl.semaphore_wait(barrier, len(partners))
    up_copies, low_copies = {}, {}
    if upper:
        for k in reversed(range(1, base)):
            up_copies[k] = send(up_send.at[flip(mine, k)], up_recv.at[k], k)
    for p in range(base_bits):
        first = (dev_bits - 1 - p) * rank
        size = rank >> p
        for q in range(1 << p):
            low_send[p][q] = staged[first + q * size:first + (q + 1) * size]
    for k in reversed(range(1, base)):
        p = top_bit(k)
        piece = lax.rem(flip(mine, k), 1 << p)
        target = low_full[0].at[0] if p == 0 else low_recv[p].at[k - (1 << p)]
        low_copies[k] = send(low_send[p].at[piece], target, k)

    for c in range(rows // 128):
        row = lax.broadcasted_iota(jnp.int32, (128, rows), 0).astype(F32) + c * 128.0
        one_hot_t[c * 128:(c + 1) * 128, :] = jnp.where(local == row, 1.0, 0.0).astype(BF16)
    chunk = rows // 4
    for c in range(4):
        at = pl.ds(c * chunk, chunk)
        ordered[at, :] = jnp.dot(one_hot[at, :], src[...], preferred_element_type=F32).astype(BF16)

    held = None
    if upper:
        for k in reversed(range(1, base)):
            up_copies[k].wait_recv()
        total = up_send[mine]
        for k in range(1, base):
            total = total + up_recv[k]
        held = total
    own_copies, above_copies = {}, {}

    def send_group(g):
        start, bits = groups[g]
        lowest = start - base_bits
        hold[g - 1][...] = held[lowest:]
        for k in reversed(range(1, 1 << bits)):
            own_copies[g, k] = send(hold[g - 1].at[top_bit(k)], recv_own[g - 1].at[k], k << start)
            if start + bits < dev_bits:
                above_copies[g, k] = send(
                    hold[g - 1].at[pl.ds(bits, dev_bits - start - bits)], recv_above[g - 1].at[k], k << start
                )

    if len(groups) > 1:
        send_group(1)

    for k in range(1, base):
        low_copies[k].wait_recv()
    low_gather = []
    for p in range(1, base_bits):
        total = low_recv[p][0]
        for k in range(1, 1 << p):
            total = total + low_recv[p][k]
        slot = lax.rem(mine, 1 << p)
        low_full[p][slot] = total
        for k in range(1, 1 << p):
            low_gather.append(send(low_full[p].at[slot], low_full[p].at[slot], k))

    lane_all = lax.broadcasted_iota(jnp.int32, (1, dev_bits * rank), 1)
    keep = jnp.zeros((1, dev_bits * rank), F32)
    for l in range(dev_bits):
        inside = (lane_all >= l * rank) & (lane_all < l * rank + ranks_ref[l])
        keep = jnp.where(inside, 1.0, keep)
    loads[3].wait()
    u_all = u[...].reshape(levels * rank, rows)
    nt = (((1,), (1,)), ((), ()))
    for c in range(4):
        at = pl.ds(c * chunk, chunk)
        u_perm[at, :] = (
            lax.dot_general(one_hot_t[at, :], u_all[: dev_bits * rank], nt, preferred_element_type=F32) * keep
        ).astype(BF16)
    loads[4].wait()
    for c in range(4):
        at = pl.ds(c * chunk, chunk)
        for g in range(rows // leaf_size):
            cols = slice(g * leaf_size, (g + 1) * leaf_size)
            mixed[at, cols] = jnp.dot(
                one_hot_t[at, cols], leaf[cols, :], preferred_element_type=F32
            ).astype(BF16)

    far_up = [None] * upper
    for g in range(1, len(groups)):
        start, bits = groups[g]
        lowest = start - base_bits
        for k in range(1, 1 << bits):
            own_copies[g, k].wait_recv()
        for j in range(bits):
            total = recv_own[g - 1][1 << j]
            for k in range((1 << j) + 1, 2 << j):
                total = total + recv_own[g - 1][k]
            far_up[lowest + j] = total
        if start + bits < dev_bits:
            for k in range(1, 1 << bits):
                above_copies[g, k].wait_recv()
            total = held[lowest + bits:]
            for k in range(1, 1 << bits):
                total = total + recv_above[g - 1][k]
            held = jnp.concatenate([held[: lowest + bits], total], axis=0)
            send_group(g + 1)
    up_gather = []
    if upper:
        for i in range(upper):
            up_full[mine, i] = far_up[i]
        for k in reversed(range(1, base)):
            up_gather.append(send(up_full.at[mine], up_full.at[mine], k))

    near_at = 0
    for l in range(dev_bits, levels):
        cluster = rows >> l - dev_bits + 1
        for g in range(rows // cluster):
            for_u = slice(g * cluster, (g + 1) * cluster)
            sib = g ^ 1
            for_v = slice(sib * cluster, (sib + 1) * cluster)
            near[near_at:near_at + rank, :] = jnp.dot(
                v_all[l * rank:(l + 1) * rank, for_v], ordered[for_v, :], preferred_element_type=F32
            ).astype(BF16)
            inside = lax.broadcasted_iota(jnp.int32, (1, rank), 1) < ranks_ref[l]
            u_near[:, near_at:near_at + rank] = (
                lax.dot_general(
                    one_hot_t[:, for_u], u_all[l * rank:(l + 1) * rank, for_u], nt, preferred_element_type=F32
                )
                * jnp.where(inside, 1.0, 0.0)
            ).astype(BF16)
            near_at += rank
    for c in range(4):
        at = pl.ds(c * chunk, chunk)
        total = jnp.dot(mixed[at, :], ordered[...], preferred_element_type=F32)
        if near_at:
            total = total + jnp.dot(u_near[at, :], near[...], preferred_element_type=F32)
        acc[at, :] = total

    for copy in low_gather:
        copy.wait_recv()
    for p in range(base_bits):
        first = (dev_bits - 1 - p) * rank
        size = rank >> p
        for q in range(1 << p):
            far[first + q * size:first + (q + 1) * size, :] = low_full[p][q]
    for copy in up_gather:
        copy.wait_recv()
    for i in range(upper):
        first = (dev_bits - 1 - (base_bits + i)) * rank
        for q in range(base):
            far[first + q * part:first + (q + 1) * part, :] = up_full[q, i]
    far_low = far[...].astype(BF16)
    stores = []
    for c in range(4):
        at = pl.ds(c * chunk, chunk)
        total = acc[at, :] + jnp.dot(u_perm[at, :], far_low, preferred_element_type=F32)
        src[at, :] = total.astype(BF16)
        copy = pltpu.make_async_copy(src.at[at], out_hbm.at[at], out_sem.at[c])
        copy.start()
        stores.append(copy)
    for copy in copies:
        copy.wait_send()
    for copy in stores:
        copy.wait()


def per_device(sources, tree_perm, leaf_blocks, u_factors, v_factors, level_ranks):
    rows, rhs = sources.shape
    leaf_size = leaf_blocks.shape[1]
    levels, rank, _ = u_factors.shape
    row_size, col_size = lax.axis_size("row"), lax.axis_size("col")
    dev_bits = (row_size * col_size).bit_length() - 1
    groups = split_bits(dev_bits)
    base_bits = groups[0][1]
    base = 1 << base_bits
    upper = dev_bits - base_bits
    part = rank // base
    cfg = (rows, rhs, leaf_size, levels, rank, row_size, col_size, groups)
    near_rows = rank * sum(2 << i for i in range(levels - dev_bits))
    vmem = pltpu.VMEM

    low = [vmem((1 << p, rank >> p, rhs), F32) for p in range(base_bits)]
    up = max(upper, 1)
    scratch = [
        vmem((rows, rhs), BF16),
        vmem(leaf_blocks.shape, BF16),
        vmem(u_factors.shape, BF16),
        vmem(v_factors.shape, BF16),
        vmem((rows, rows), BF16),
        vmem((rows, rows), BF16),
        vmem((rows, rhs), BF16),
        vmem((rows, rows), BF16),
        vmem((rows, dev_bits * rank), BF16),
        vmem((rows, max(near_rows, rank)), BF16),
        vmem((max(near_rows, rank), rhs), BF16),
        vmem((rows, rhs), F32),
        vmem((dev_bits * rank, rhs), F32),
        vmem((dev_bits * rank, rhs), F32),
    ]
    scratch += low + low + low
    scratch += [vmem((base, up, part, rhs), F32)] * 3
    scratch += [vmem((dev_bits - start, part, rhs), F32) for start, _ in groups[1:]]
    scratch += [vmem((1 << bits, part, rhs), F32) for _, bits in groups[1:]]
    scratch += [
        vmem((1 << bits, max(dev_bits - start - bits, 1), part, rhs), F32) for start, bits in groups[1:]
    ]
    total = (3 if upper else 1) * base + base + 2 * sum(1 << bits for _, bits in groups[1:])
    scratch += [
        pltpu.SemaphoreType.DMA((5,)),
        pltpu.SemaphoreType.DMA((4,)),
        pltpu.SemaphoreType.DMA((total,)),
        pltpu.SemaphoreType.DMA((total,)),
    ]
    any_space = pl.BlockSpec(memory_space=pl.ANY)
    return pl.pallas_call(
        functools.partial(kernel, cfg),
        out_shape=jax.ShapeDtypeStruct((rows, rhs), BF16),
        in_specs=[
            pl.BlockSpec(memory_space=pltpu.SMEM),
            pl.BlockSpec(memory_space=pltpu.VMEM),
            any_space, any_space, any_space, any_space,
        ],
        out_specs=any_space,
        scratch_shapes=scratch,
        compiler_params=pltpu.CompilerParams(
            collective_id=0, has_side_effects=True, vmem_limit_bytes=56 * 1024 * 1024
        ),
    )(level_ranks, tree_perm.reshape(1, rows), sources, leaf_blocks, u_factors, v_factors)


def solution(mesh):
    placed = (
        P(("row", "col"), None),
        P(("row", "col")),
        P(("row", "col"), None),
        P(None, None, ("row", "col")),
        P(None, None, ("row", "col")),
        P(),
    )
    return jax.shard_map(
        per_device, mesh=mesh, in_specs=placed, out_specs=P(("row", "col"), None), check_vma=False
    )
```

time: 57.3 us -> 23.1 us (0.40)
  Pallas kernels: 0 us -> 20.4 us
  local copies, waits for them, and re-layouts: 22.6 us -> 2.49 us
  starting transfers between devices: 14.7 us -> 0 us
  matrix products: 10.4 us -> 0 us
  waiting for transfers between devices: 5.07 us -> 0 us
  blocking collectives: 2.74 us -> 0 us
  other arithmetic: 1.2 us -> 0 us
    pallas_call x0 -> x1, Pallas kernels: none -> 20.4 us  [per_device(): pl.pallas_call(functools.partial(kernel, cfg), out_shape=jax.ShapeDtypeSt...]
    ppermute x11 -> x0, starting transfers between devices: 14.7 us -> none  [partner(): lax.ppermute(x, axis, [(i, i ^ 1 << distance) for i in range(lax.axis_siz...]
    dot_general x5 -> x0, matrix products: 10.4 us -> none  [the longest x1 3.71 us: per_device(): jnp.einsum('gij,gjr->gir', leaf_blocks.reshape(leaf_count, leaf_size, lea...]
    scatter x1 -> x0, local copies, waits for them, and re-layouts: 6.79 us -> none  [per_device(): jnp.zeros_like(sources).at[local_index].set(result.astype(jnp.bfloat16))]
    reshape x2 -> x0, local copies, waits for them, and re-layouts: 6.53 us -> none  [the longest x1 3.28 us: per_device(): result = result + jnp.einsum('kgs,gkr->gsr', u_factors[level].reshape(ran...]
    ppermute x11 -> x0, waiting for transfers between devices: 5.07 us -> none  [partner(): lax.ppermute(x, axis, [(i, i ^ 1 << distance) for i in range(lax.axis_siz...]
    gather x1 -> x0, local copies, waits for them, and re-layouts: 4.02 us -> none  [per_device(): ordered = sources[local_index]]
    all_gather x1 -> x0, blocking collectives: 2.74 us -> none  [per_device(): coarse_stack = lax.all_gather(coarse_stack, 'col', axis=2, tiled=True)]
  transfers between devices with their start and end apart: 11 -> 0, of which waited for: 4 -> 0; matrix products, arithmetic and copies ran while one was open for 26% -> 0% of each run, Pallas kernels for 0% -> 0%
where the time goes in v1:
time: 23.1 us; the launch traced here: 22.9 us
  Pallas kernels  20.4 us (88%)
  local copies, waits for them, and re-layouts  2.49 us (11%)
    pallas_call x1, Pallas kernels, per_device(): pl.pallas_call(functools.partial(kernel, cfg), out_shape=jax.ShapeDtypeSt...  20.4 us
    unnamed x1, local copies, waits for them, and re-layouts  2.49 us

profile of v1, /device:TPU:0, one launch (start us, length us, event | category | flops | bytes accessed | tf_op | source)
XLA Modules:
  0.0 22.9 jit_solution(14447160235401021692)
XLA Ops:
  0.0 20.4 %shard_map.64 = bf16[1024,640]{1,0:T(8,128)(2,1)} custom-call(s32[6]{0:T(128)} %ranks_ref.1, s32[1,1024]{1,0:T(1,128)} %bitcast.1, bf16[1024,640]{1,0:T(8,128)(2,1)} %src_hbm.1, bf16[1024,512]{1,0:T(8,128)(2,1)} %leaf_hbm.1, bf16[6,32,1024]{2,1,0:T(8,128)(2,1)} %u_hbm.1, bf16[6,32,1024]{2,1,0:T(8,128)(2,1)} %v_hbm.1), custom_call_target="tpu_custom_call" | custom-call | tf_op jit(solution)/shard_map/pallas_call | solution.py:330
  20.4 2.5 %copy.8 = bf16[1024,640]{1,0:T(8,128)(2,1)} copy(bf16[1024,640]{1,0:T(8,128)(2,1)} %shard_map.64) | data formatting | bytes 2621440

commit v2 on v1

v2 whole, which is shorter than its diff:
```python
import functools

import jax
import jax.numpy as jnp
from jax import lax
from jax.experimental import pallas as pl
from jax.experimental.pallas import tpu as pltpu
from jax.sharding import PartitionSpec as P

F32 = jnp.float32
BF16 = jnp.bfloat16
VMEM_BYTES = 67043328


def flip(x, mask):
    bit = 0
    while mask >> bit:
        if mask >> bit & 1:
            x = x + (1 << bit) * (1 - 2 * lax.rem(lax.div(x, 1 << bit), 2))
        bit += 1
    return x


def split_bits(dev_bits):
    groups, start = [], 0
    while start < dev_bits:
        bits = min(3, dev_bits - start)
        groups.append((start, bits))
        start += bits
    return groups


def top_bit(k):
    return k.bit_length() - 1


def kernel(
    cfg,
    ranks_ref, perm_ref, src_hbm, leaf_hbm, u_hbm, v_hbm,
    acc, u_perm, far,
    src, leaf, u, v, one_hot, one_hot_t, ordered, mixed, u_near, near, staged,
    *rest,
):
    rows, rhs, leaf_size, levels, rank, row_size, col_size, groups = cfg
    dev_bits = sum(bits for _, bits in groups)
    base_bits = groups[0][1]
    base = 1 << base_bits
    upper = dev_bits - base_bits
    part = rank // base
    rest = list(rest)
    low_send = [rest.pop(0) for _ in range(base_bits)]
    low_recv = [rest.pop(0) for _ in range(base_bits)]
    low_full = [rest.pop(0) for _ in range(base_bits)]
    up_send, up_recv, up_full = [rest.pop(0) for _ in range(3)]
    hold = [rest.pop(0) for _ in groups[1:]]
    recv_own = [rest.pop(0) for _ in groups[1:]]
    recv_above = [rest.pop(0) for _ in groups[1:]]
    in_sem, send_sem, recv_sem = rest

    me = lax.axis_index("row") * col_size + lax.axis_index("col")
    mine = lax.rem(me, base)

    loads = []
    half = rows // 2
    for at, (a, b) in enumerate(
        [(v_hbm, v)]
        + [(src_hbm.at[pl.ds(h * half, half)], src.at[pl.ds(h * half, half)]) for h in range(2)]
        + [(u_hbm, u), (leaf_hbm, leaf)]
    ):
        copy = pltpu.make_async_copy(a, b, in_sem.at[at])
        copy.start()
        loads.append(copy)

    barrier = pltpu.get_barrier_semaphore()
    partners = [k << start for start, bits in groups for k in range(1, 1 << bits)]

    def device(mask):
        other = flip(me, mask)
        return (lax.div(other, col_size), lax.rem(other, col_size))

    for mask in partners:
        pl.semaphore_signal(
            barrier, inc=1, device_id=device(mask), device_id_type=pl.DeviceIdType.MESH
        )

    count = [0]
    copies = []

    def send(source, target, mask):
        at = count[0]
        count[0] += 1
        copy = pltpu.make_async_remote_copy(
            src_ref=source,
            dst_ref=target,
            send_sem=send_sem.at[at],
            recv_sem=recv_sem.at[at],
            device_id=device(mask),
            device_id_type=pl.DeviceIdType.MESH,
        )
        copy.start()
        copies.append(copy)
        return copy

    local = (perm_ref[...] - me * rows).astype(F32)
    wide = jnp.broadcast_to(local, (128, rows)).T
    lane = lax.broadcasted_iota(jnp.int32, (rows, 128), 1).astype(F32)
    for c in range(rows // 128):
        one_hot[:, c * 128:(c + 1) * 128] = jnp.where(wide == lane + c * 128.0, 1.0, 0.0).astype(BF16)

    loads[0].wait()
    v_all = v[...].reshape(levels * rank, rows)
    v_perm = jnp.dot(v_all[: dev_bits * rank], one_hot[...], preferred_element_type=F32).astype(BF16)
    loads[1].wait()
    loads[2].wait()
    coef = jnp.dot(v_perm, src[...], preferred_element_type=F32)
    staged[...] = coef
    for p in range(base_bits, dev_bits):
        first = (dev_bits - 1 - p) * rank
        for q in range(base):
            up_send[p - base_bits, q] = staged[first + q * part:first + (q + 1) * part]

    pl.semaphore_wait(barrier, len(partners))
    up_copies, low_copies = {}, {}
    if upper:
        for i in reversed(range(upper)):
            for k in reversed(range(1, base)):
                up_copies[i, k] = send(up_send.at[i, flip(mine, k)], up_recv.at[i, k], k)
    for p in range(base_bits):
        first = (dev_bits - 1 - p) * rank
        size = rank >> p
        for q in range(1 << p):
            low_send[p][q] = staged[first + q * size:first + (q + 1) * size]
    for k in reversed(range(1, base)):
        p = top_bit(k)
        piece = lax.rem(flip(mine, k), 1 << p)
        target = low_full[0].at[0] if p == 0 else low_recv[p].at[k - (1 << p)]
        low_copies[k] = send(low_send[p].at[piece], target, k)

    for c in range(rows // 128):
        row = lax.broadcasted_iota(jnp.int32, (128, rows), 0).astype(F32) + c * 128.0
        one_hot_t[c * 128:(c + 1) * 128, :] = jnp.where(local == row, 1.0, 0.0).astype(BF16)
    chunk = rows // 4
    for c in range(4):
        at = pl.ds(c * chunk, chunk)
        ordered[at, :] = jnp.dot(one_hot[at, :], src[...], preferred_element_type=F32).astype(BF16)

    own_copies, above_copies, up_gather = {}, {}, {}

    def plane_sum(i):
        for k in reversed(range(1, base)):
            up_copies[i, k].wait_recv()
        total = up_send[i, mine]
        for k in range(1, base):
            total = total + up_recv[i, k]
        return total

    def send_group(g, i, value):
        start, bits = groups[g]
        at = i - (start - base_bits)
        hold[g - 1][at] = value
        if at < bits:
            for k in reversed(range(1 << at, 2 << at)):
                own_copies[g, k] = send(hold[g - 1].at[at], recv_own[g - 1].at[k], k << start)
        else:
            for k in reversed(range(1, 1 << bits)):
                above_copies[g, i, k] = send(
                    hold[g - 1].at[at], recv_above[g - 1].at[at - bits, k], k << start
                )

    def gather_level(g, j):
        i = groups[g][0] - base_bits + j
        total = None
        for k in range(1 << j, 2 << j):
            own_copies[g, k].wait_recv()
            total = recv_own[g - 1][k] if total is None else total + recv_own[g - 1][k]
        up_full[i, mine] = total
        for k in reversed(range(1, base)):
            up_gather[i, k] = send(up_full.at[i, mine], up_full.at[i, mine], k)

    for i in reversed(range(upper)):
        send_group(1, i, plane_sum(i))

    lane_all = lax.broadcasted_iota(jnp.int32, (1, dev_bits * rank), 1)
    keep = jnp.zeros((1, dev_bits * rank), F32)
    for l in range(dev_bits):
        inside = (lane_all >= l * rank) & (lane_all < l * rank + ranks_ref[l])
        keep = jnp.where(inside, 1.0, keep)
    loads[3].wait()
    u_all = u[...].reshape(levels * rank, rows)
    nt = (((1,), (1,)), ((), ()))
    for c in range(4):
        at = pl.ds(c * chunk, chunk)
        u_perm[at, :] = (
            lax.dot_general(one_hot_t[at, :], u_all[: dev_bits * rank], nt, preferred_element_type=F32) * keep
        ).astype(BF16)
    loads[4].wait()

    def mix():
        for c in range(4):
            at = pl.ds(c * chunk, chunk)
            for g in range(rows // leaf_size):
                cols = slice(g * leaf_size, (g + 1) * leaf_size)
                mixed[at, cols] = jnp.dot(
                    one_hot_t[at, cols], leaf[cols, :], preferred_element_type=F32
                ).astype(BF16)

    low_gather = []

    def low_levels():
        for k in range(1, base):
            low_copies[k].wait_recv()
        for p in range(1, base_bits):
            total = low_recv[p][0]
            for k in range(1, 1 << p):
                total = total + low_recv[p][k]
            slot = lax.rem(mine, 1 << p)
            low_full[p][slot] = total
            for k in range(1, 1 << p):
                low_gather.append(send(low_full[p].at[slot], low_full[p].at[slot], k))

    def near_levels():
        near_at = 0
        for l in range(dev_bits, levels):
            cluster = rows >> l - dev_bits + 1
            for g in range(rows // cluster):
                for_u = slice(g * cluster, (g + 1) * cluster)
                sib = g ^ 1
                for_v = slice(sib * cluster, (sib + 1) * cluster)
                near[near_at:near_at + rank, :] = jnp.dot(
                    v_all[l * rank:(l + 1) * rank, for_v], ordered[for_v, :], preferred_element_type=F32
                ).astype(BF16)
                inside = lax.broadcasted_iota(jnp.int32, (1, rank), 1) < ranks_ref[l]
                u_near[:, near_at:near_at + rank] = (
                    lax.dot_general(
                        one_hot_t[:, for_u], u_all[l * rank:(l + 1) * rank, for_u], nt, preferred_element_type=F32
                    )
                    * jnp.where(inside, 1.0, 0.0)
                ).astype(BF16)
                near_at += rank

    def apply_rows(c):
        at = pl.ds(c * chunk, chunk)
        total = jnp.dot(mixed[at, :], ordered[...], preferred_element_type=F32)
        if levels > dev_bits:
            total = total + jnp.dot(u_near[at, :], near[...], preferred_element_type=F32)
        acc[at, :] = total

    fillers = [mix, low_levels, near_levels] + [functools.partial(apply_rows, c) for c in range(4)]
    fillers.pop(0)()
    for g in range(1, len(groups)):
        start, bits = groups[g]
        for i in reversed(range(start + bits - base_bits, upper)):
            total = hold[g - 1][i - (start - base_bits)]
            for k in reversed(range(1, 1 << bits)):
                above_copies[g, i, k].wait_recv()
                total = total + recv_above[g - 1][i - (start + bits - base_bits), k]
            send_group(g + 1, i, total)
        for j in range(bits):
            gather_level(g, j)
            for _ in range(2):
                if fillers and j < bits - 1:
                    fillers.pop(0)()
    for filler in fillers:
        filler()

    for copy in low_gather:
        copy.wait_recv()
    for p in range(base_bits):
        first = (dev_bits - 1 - p) * rank
        size = rank >> p
        for q in range(1 << p):
            staged[first + q * size:first + (q + 1) * size, :] = low_full[p][q]
    for i in range(upper):
        for k in range(1, base):
            up_gather[i, k].wait_recv()
        first = (dev_bits - 1 - (base_bits + i)) * rank
        for q in range(base):
            staged[first + q * part:first + (q + 1) * part, :] = up_full[i, q]
    far[...] = staged[...].astype(BF16)
    for copy in copies:
        copy.wait_send()


def finish(acc, u_perm, far, out_hbm, out, out_sem):
    chunk = acc.shape[0] // 4
    stores = []
    for c in range(4):
        at = pl.ds(c * chunk, chunk)
        total = acc[at, :] + jnp.dot(u_perm[at, :], far[...], preferred_element_type=F32)
        out[at, :] = total.astype(BF16)
        copy = pltpu.make_async_copy(out.at[at], out_hbm.at[at], out_sem.at[c])
        copy.start()
        stores.append(copy)
    for copy in stores:
        copy.wait()


def per_device(sources, tree_perm, leaf_blocks, u_factors, v_factors, level_ranks):
    rows, rhs = sources.shape
    leaf_size = leaf_blocks.shape[1]
    levels, rank, _ = u_factors.shape
    row_size, col_size = lax.axis_size("row"), lax.axis_size("col")
    dev_bits = (row_size * col_size).bit_length() - 1
    groups = split_bits(dev_bits)
    base_bits = groups[0][1]
    base = 1 << base_bits
    upper = dev_bits - base_bits
    part = rank // base
    cfg = (rows, rhs, leaf_size, levels, rank, row_size, col_size, groups)
    near_rows = rank * sum(2 << i for i in range(levels - dev_bits))
    vmem = pltpu.VMEM

    low = [vmem((1 << p, rank >> p, rhs), F32) for p in range(base_bits)]
    up = max(upper, 1)
    scratch = [
        vmem((rows, rhs), BF16),
        vmem(leaf_blocks.shape, BF16),
        vmem(u_factors.shape, BF16),
        vmem(v_factors.shape, BF16),
        vmem((rows, rows), BF16),
        vmem((rows, rows), BF16),
        vmem((rows, rhs), BF16),
        vmem((rows, rows), BF16),
        vmem((rows, max(near_rows, rank)), BF16),
        vmem((max(near_rows, rank), rhs), BF16),
        vmem((dev_bits * rank, rhs), F32),
    ]
    scratch += low + low + low
    scratch += [vmem((up, base, part, rhs), F32)] * 3
    scratch += [vmem((dev_bits - start, part, rhs), F32) for start, _ in groups[1:]]
    scratch += [vmem((1 << bits, part, rhs), F32) for _, bits in groups[1:]]
    scratch += [
        vmem((max(dev_bits - start - bits, 1), 1 << bits, part, rhs), F32) for start, bits in groups[1:]
    ]
    total = (2 * upper + 2) * base + sum((dev_bits - start) << bits for start, bits in groups[1:])
    scratch += [
        pltpu.SemaphoreType.DMA((5,)),
        pltpu.SemaphoreType.DMA((total,)),
        pltpu.SemaphoreType.DMA((total,)),
    ]
    wide = -(-dev_bits * rank // 128) * 128
    kept = rows * rhs * 4 + rows * wide * 2 + dev_bits * rank * rhs * 2
    any_space = pl.BlockSpec(memory_space=pl.ANY)
    vmem_space = pl.BlockSpec(memory_space=pltpu.VMEM)
    acc, u_perm, far = pl.pallas_call(
        functools.partial(kernel, cfg),
        out_shape=(
            pltpu.VMEM((rows, rhs), F32),
            pltpu.VMEM((rows, dev_bits * rank), BF16),
            pltpu.VMEM((dev_bits * rank, rhs), BF16),
        ),
        in_specs=[
            pl.BlockSpec(memory_space=pltpu.SMEM), vmem_space,
            any_space, any_space, any_space, any_space,
        ],
        out_specs=(vmem_space, vmem_space, vmem_space),
        scratch_shapes=scratch,
        compiler_params=pltpu.CompilerParams(
            collective_id=0, has_side_effects=True, vmem_limit_bytes=VMEM_BYTES - kept - 96 * 1024
        ),
    )(level_ranks, tree_perm.reshape(1, rows), sources, leaf_blocks, u_factors, v_factors)
    return pl.pallas_call(
        finish,
        out_shape=jax.ShapeDtypeStruct((rows, rhs), BF16),
        in_specs=[vmem_space, vmem_space, vmem_space],
        out_specs=any_space,
        scratch_shapes=[vmem((rows, rhs), BF16), pltpu.SemaphoreType.DMA((4,))],
        compiler_params=pltpu.CompilerParams(vmem_limit_bytes=8 * 1024 * 1024),
    )(acc, u_perm, far)


def solution(mesh):
    placed = (
        P(("row", "col"), None),
        P(("row", "col")),
        P(("row", "col"), None),
        P(None, None, ("row", "col")),
        P(None, None, ("row", "col")),
        P(),
    )
    return jax.shard_map(
        per_device, mesh=mesh, in_specs=placed, out_specs=P(("row", "col"), None), check_vma=False
    )
```

time: 23.1 us -> 20.1 us (0.87)
  local copies, waits for them, and re-layouts: 2.49 us -> 0 us
  Pallas kernels: 20.4 us -> 19.9 us
    unnamed x1 -> x0, local copies, waits for them, and re-layouts: 2.49 us -> none
    pallas_call x1 -> x2, Pallas kernels: 20.4 us -> 19.9 us  [the longest x1 18.5 us: per_device(): pl.pallas_call(functools.partial(kernel, cfg), out_shape=(pltpu.VMEM((row...]
where the time goes in v2:
time: 20.1 us; the launch traced here: 19.9 us
  Pallas kernels  19.9 us (99%)
    pallas_call x1, Pallas kernels, per_device(): pl.pallas_call(functools.partial(kernel, cfg), out_shape=(pltpu.VMEM((row...  18.5 us
    pallas_call x1, Pallas kernels, per_device(): pl.pallas_call(finish, out_shape=jax.ShapeDtypeStruct((rows, rhs), BF16),...  1.37 us

profile of v2, /device:TPU:0, one launch (start us, length us, event | category | flops | bytes accessed | tf_op | source)
XLA Modules:
  0.0 19.9 jit_solution(2998493764341054734)
XLA Ops:
  0.0 18.5 %shard_map.64 = (f32[1024,640]{1,0:T(8,128)S(1)}, bf16[1024,160]{1,0:T(8,128)(2,1)S(1)}, bf16[160,640]{1,0:T(8,128)(2,1)S(1)}) custom-call(s32[6]{0:T(128)} %ranks_ref.1, s32[1,1024]{1,0:T(1,128)} %bitcast.1, bf16[1024,640]{1,0:T(8,128)(2,1)} %src_hbm.1, bf16[1024,512]{1,0:T(8,128)(2,1)} %leaf_hbm.1, bf16[6,32,1024]{2,1,0:T(8,128)(2,1)} %u_hbm.1, ...), custom_call_target="tpu_custom_call" | custom-call | tf_op jit(solution)/shard_map/pallas_call | solution.py:345
  18.5 1.4 %shard_map.65 = bf16[1024,640]{1,0:T(8,128)(2,1)} custom-call(f32[1024,640]{1,0:T(8,128)S(1)} %get-tuple-element.8.acc, bf16[1024,160]{1,0:T(8,128)(2,1)S(1)} %get-tuple-element.9.u_perm, bf16[160,640]{1,0:T(8,128)(2,1)S(1)} %get-tuple-element.10.far), custom_call_target="tpu_custom_call" | custom-call | tf_op jit(solution)/shard_map/pallas_call | solution.py:362

commit v3 on v2

--- a/solution.py
+++ b/solution.py
@@ -36,7 +36,7 @@
 
 def kernel(
     cfg,
-    ranks_ref, perm_ref, src_hbm, leaf_hbm, u_hbm, v_hbm,
+    ranks_hbm, perm_hbm, src_hbm, leaf_hbm, u_hbm, v_hbm,
     acc, u_perm, far,
     src, leaf, u, v, one_hot, one_hot_t, ordered, mixed, u_near, near, staged,
     *rest,
@@ -51,25 +51,28 @@
     low_send = [rest.pop(0) for _ in range(base_bits)]
     low_recv = [rest.pop(0) for _ in range(base_bits)]
     low_full = [rest.pop(0) for _ in range(base_bits)]
+    low_chip = [rest.pop(0) for _ in range(base_bits)]
+    low_sum = [rest.pop(0) for _ in range(base_bits)]
     up_send, up_recv, up_full = [rest.pop(0) for _ in range(3)]
     hold = [rest.pop(0) for _ in groups[1:]]
     recv_own = [rest.pop(0) for _ in groups[1:]]
     recv_above = [rest.pop(0) for _ in groups[1:]]
-    in_sem, send_sem, recv_sem = rest
+    ranks_ref, perm_ref, in_sem, send_sem, recv_sem = rest
 
     me = lax.axis_index("row") * col_size + lax.axis_index("col")
     mine = lax.rem(me, base)
 
-    loads = []
     half = rows // 2
-    for at, (a, b) in enumerate(
-        [(v_hbm, v)]
-        + [(src_hbm.at[pl.ds(h * half, half)], src.at[pl.ds(h * half, half)]) for h in range(2)]
-        + [(u_hbm, u), (leaf_hbm, leaf)]
-    ):
-        copy = pltpu.make_async_copy(a, b, in_sem.at[at])
+    loads = [
+        pltpu.make_async_copy(a, b, in_sem.at[at])
+        for at, (a, b) in enumerate(
+            [(perm_hbm, perm_ref), (v_hbm, v)]
+            + [(src_hbm.at[pl.ds(h * half, half)], src.at[pl.ds(h * half, half)]) for h in range(2)]
+            + [(ranks_hbm, ranks_ref), (u_hbm, u), (leaf_hbm, leaf)]
+        )
+    ]
+    for copy in loads[:4]:
         copy.start()
-        loads.append(copy)
 
     barrier = pltpu.get_barrier_semaphore()
     partners = [k << start for start, bits in groups for k in range(1, 1 << bits)]
@@ -101,17 +104,20 @@
         copies.append(copy)
         return copy
 
+    loads[0].wait()
     local = (perm_ref[...] - me * rows).astype(F32)
     wide = jnp.broadcast_to(local, (128, rows)).T
     lane = lax.broadcasted_iota(jnp.int32, (rows, 128), 1).astype(F32)
     for c in range(rows // 128):
         one_hot[:, c * 128:(c + 1) * 128] = jnp.where(wide == lane + c * 128.0, 1.0, 0.0).astype(BF16)
 
-    loads[0].wait()
+    loads[1].wait()
     v_all = v[...].reshape(levels * rank, rows)
     v_perm = jnp.dot(v_all[: dev_bits * rank], one_hot[...], preferred_element_type=F32).astype(BF16)
-    loads[1].wait()
     loads[2].wait()
+    loads[3].wait()
+    for copy in loads[4:]:
+        copy.start()
     coef = jnp.dot(v_perm, src[...], preferred_element_type=F32)
     staged[...] = coef
     for p in range(base_bits, dev_bits):
@@ -125,24 +131,39 @@
         for i in reversed(range(upper)):
             for k in reversed(range(1, base)):
                 up_copies[i, k] = send(up_send.at[i, flip(mine, k)], up_recv.at[i, k], k)
+    chip_copies = {}
+    bit = lax.rem(me, 2)
     for p in range(base_bits):
         first = (dev_bits - 1 - p) * rank
         size = rank >> p
+        if p == 0:
+            low_send[0][0] = staged[first:first + size]
+            low_copies[1] = send(low_send[0].at[0], low_full[0].at[0], 1)
+            continue
         for q in range(1 << p):
-            low_send[p][q] = staged[first + q * size:first + (q + 1) * size]
-    for k in reversed(range(1, base)):
-        p = top_bit(k)
-        piece = lax.rem(flip(mine, k), 1 << p)
-        target = low_full[0].at[0] if p == 0 else low_recv[p].at[k - (1 << p)]
-        low_copies[k] = send(low_send[p].at[piece], target, k)
+            low_send[p][q % 2, q // 2] = staged[first + q * size:first + (q + 1) * size]
+        chip_copies[p] = send(low_send[p].at[1 - bit], low_chip[p], 1)
 
     for c in range(rows // 128):
         row = lax.broadcasted_iota(jnp.int32, (128, rows), 0).astype(F32) + c * 128.0
         one_hot_t[c * 128:(c + 1) * 128, :] = jnp.where(local == row, 1.0, 0.0).astype(BF16)
     chunk = rows // 4
-    for c in range(4):
+
+    def order_rows(c):
         at = pl.ds(c * chunk, chunk)
         ordered[at, :] = jnp.dot(one_hot[at, :], src[...], preferred_element_type=F32).astype(BF16)
+
+    order_rows(0)
+    order_rows(1)
+
+    for p in range(1, base_bits):
+        chip_copies[p].wait_recv()
+        low_sum[p][...] = low_send[p][bit] + low_chip[p][...]
+        for k in reversed(range(1 << p, 2 << p, 2)):
+            piece = lax.div(lax.rem(flip(mine, k), 1 << p), 2)
+            low_copies[k] = send(low_sum[p].at[piece], low_recv[p].at[(k - (1 << p)) // 2], k)
+    order_rows(2)
+    order_rows(3)
 
     own_copies, above_copies, up_gather = {}, {}, {}
 
@@ -180,12 +201,13 @@
     for i in reversed(range(upper)):
         send_group(1, i, plane_sum(i))
 
+    loads[4].wait()
     lane_all = lax.broadcasted_iota(jnp.int32, (1, dev_bits * rank), 1)
     keep = jnp.zeros((1, dev_bits * rank), F32)
     for l in range(dev_bits):
         inside = (lane_all >= l * rank) & (lane_all < l * rank + ranks_ref[l])
         keep = jnp.where(inside, 1.0, keep)
-    loads[3].wait()
+    loads[5].wait()
     u_all = u[...].reshape(levels * rank, rows)
     nt = (((1,), (1,)), ((), ()))
     for c in range(4):
@@ -193,7 +215,7 @@
         u_perm[at, :] = (
             lax.dot_general(one_hot_t[at, :], u_all[: dev_bits * rank], nt, preferred_element_type=F32) * keep
         ).astype(BF16)
-    loads[4].wait()
+    loads[6].wait()
 
     def mix():
         for c in range(4):
@@ -207,11 +229,11 @@
     low_gather = []
 
     def low_levels():
-        for k in range(1, base):
-            low_copies[k].wait_recv()
+        for copy in low_copies.values():
+            copy.wait_recv()
         for p in range(1, base_bits):
             total = low_recv[p][0]
-            for k in range(1, 1 << p):
+            for k in range(1, 1 << p - 1):
                 total = total + low_recv[p][k]
             slot = lax.rem(mine, 1 << p)
             low_full[p][slot] = total
@@ -311,6 +333,8 @@
     vmem = pltpu.VMEM
 
     low = [vmem((1 << p, rank >> p, rhs), F32) for p in range(base_bits)]
+    low_pairs = [vmem((1, rank, rhs), F32)] + [vmem((2, 1 << p - 1, rank >> p, rhs), F32) for p in range(1, base_bits)]
+    low_half = [vmem((max(1 << p >> 1, 1), rank >> p, rhs), F32) for p in range(base_bits)]
     up = max(upper, 1)
     scratch = [
         vmem((rows, rhs), BF16),
@@ -325,7 +349,7 @@
         vmem((max(near_rows, rank), rhs), BF16),
         vmem((dev_bits * rank, rhs), F32),
     ]
-    scratch += low + low + low
+    scratch += low_pairs + low_half + low + low_half + low_half
     scratch += [vmem((up, base, part, rhs), F32)] * 3
     scratch += [vmem((dev_bits - start, part, rhs), F32) for start, _ in groups[1:]]
     scratch += [vmem((1 << bits, part, rhs), F32) for _, bits in groups[1:]]
@@ -334,7 +358,9 @@
     ]
     total = (2 * upper + 2) * base + sum((dev_bits - start) << bits for start, bits in groups[1:])
     scratch += [
-        pltpu.SemaphoreType.DMA((5,)),
+        pltpu.SMEM(level_ranks.shape, jnp.int32),
+        vmem((1, rows), jnp.int32),
+        pltpu.SemaphoreType.DMA((7,)),
         pltpu.SemaphoreType.DMA((total,)),
         pltpu.SemaphoreType.DMA((total,)),
     ]
@@ -349,10 +375,7 @@
             pltpu.VMEM((rows, dev_bits * rank), BF16),
             pltpu.VMEM((dev_bits * rank, rhs), BF16),
         ),
-        in_specs=[
-            pl.BlockSpec(memory_space=pltpu.SMEM), vmem_space,
-            any_space, any_space, any_space, any_space,
-        ],
+        in_specs=[any_space] * 6,
         out_specs=(vmem_space, vmem_space, vmem_space),
         scratch_shapes=scratch,
         compiler_params=pltpu.CompilerParams(

time: 20.1 us -> 18.8 us (0.935)
  Pallas kernels: 19.9 us -> 18.6 us
    pallas_call x1, Pallas kernels: 18.5 us -> 17.2 us  [per_device(): pl.pallas_call(functools.partial(kernel, cfg), out_shape=(pltpu.VMEM((row...]
where the time goes in v3:
time: 18.8 us; the launch traced here: 18.6 us
  Pallas kernels  18.6 us (99%)
    pallas_call x1, Pallas kernels, per_device(): pl.pallas_call(functools.partial(kernel, cfg), out_shape=(pltpu.VMEM((row...  17.2 us
    pallas_call x1, Pallas kernels, per_device(): pl.pallas_call(finish, out_shape=jax.ShapeDtypeStruct((rows, rhs), BF16),...  1.37 us

profile of v3, /device:TPU:0, one launch (start us, length us, event | category | flops | bytes accessed | tf_op | source)
XLA Modules:
  0.0 18.6 jit_solution(4848777515991837313)
XLA Ops:
  0.0 17.2 %shard_map.64 = (f32[1024,640]{1,0:T(8,128)S(1)}, bf16[1024,160]{1,0:T(8,128)(2,1)S(1)}, bf16[160,640]{1,0:T(8,128)(2,1)S(1)}) custom-call(s32[6]{0:T(128)} %ranks_hbm.1, s32[1,1024]{1,0:T(1,128)} %bitcast.1, bf16[1024,640]{1,0:T(8,128)(2,1)} %src_hbm.1, bf16[1024,512]{1,0:T(8,128)(2,1)} %leaf_hbm.1, bf16[6,32,1024]{2,1,0:T(8,128)(2,1)} %u_hbm.1, ...), custom_call_target="tpu_custom_call" | custom-call | tf_op jit(solution)/shard_map/pallas_call | solution.py:371
  17.2 1.4 %shard_map.65 = bf16[1024,640]{1,0:T(8,128)(2,1)} custom-call(f32[1024,640]{1,0:T(8,128)S(1)} %get-tuple-element.8.acc, bf16[1024,160]{1,0:T(8,128)(2,1)S(1)} %get-tuple-element.9.u_perm, bf16[160,640]{1,0:T(8,128)(2,1)S(1)} %get-tuple-element.10.far), custom_call_target="tpu_custom_call" | custom-call | tf_op jit(solution)/shard_map/pallas_call | solution.py:385

commit v4 on v3

--- a/solution.py
+++ b/solution.py
@@ -120,17 +120,14 @@
         copy.start()
     coef = jnp.dot(v_perm, src[...], preferred_element_type=F32)
     staged[...] = coef
-    for p in range(base_bits, dev_bits):
-        first = (dev_bits - 1 - p) * rank
-        for q in range(base):
-            up_send[p - base_bits, q] = staged[first + q * part:first + (q + 1) * part]
-
     pl.semaphore_wait(barrier, len(partners))
     up_copies, low_copies = {}, {}
-    if upper:
-        for i in reversed(range(upper)):
-            for k in reversed(range(1, base)):
-                up_copies[i, k] = send(up_send.at[i, flip(mine, k)], up_recv.at[i, k], k)
+    for i in reversed(range(upper)):
+        first = (upper - 1 - i) * rank
+        for q in range(base):
+            up_send[i, q] = staged[first + q * part:first + (q + 1) * part]
+        for k in reversed(range(1, base)):
+            up_copies[i, k] = send(up_send.at[i, flip(mine, k)], up_recv.at[i, k], k)
     chip_copies = {}
     bit = lax.rem(me, 2)
     for p in range(base_bits):
@@ -279,9 +276,8 @@
             send_group(g + 1, i, total)
         for j in range(bits):
             gather_level(g, j)
-            for _ in range(2):
-                if fillers and j < bits - 1:
-                    fillers.pop(0)()
+            if low_levels in fillers and j < bits - 1:
+                fillers.pop(0)()
     for filler in fillers:
         filler()
 
@@ -304,9 +300,9 @@
 
 
 def finish(acc, u_perm, far, out_hbm, out, out_sem):
-    chunk = acc.shape[0] // 4
+    chunk = acc.shape[0] // 8
     stores = []
-    for c in range(4):
+    for c in range(8):
         at = pl.ds(c * chunk, chunk)
         total = acc[at, :] + jnp.dot(u_perm[at, :], far[...], preferred_element_type=F32)
         out[at, :] = total.astype(BF16)
@@ -387,7 +383,7 @@
         out_shape=jax.ShapeDtypeStruct((rows, rhs), BF16),
         in_specs=[vmem_space, vmem_space, vmem_space],
         out_specs=any_space,
-        scratch_shapes=[vmem((rows, rhs), BF16), pltpu.SemaphoreType.DMA((4,))],
+        scratch_shapes=[vmem((rows, rhs), BF16), pltpu.SemaphoreType.DMA((8,))],
         compiler_params=pltpu.CompilerParams(vmem_limit_bytes=8 * 1024 * 1024),
     )(acc, u_perm, far)
 

time: 18.8 us -> 18.8 us (level)
  no operation moved by 1% of the time
where the time goes in v4:
time: 18.8 us; the launch traced here: 18.7 us
  Pallas kernels  18.6 us (99%)
    pallas_call x1, Pallas kernels, per_device(): pl.pallas_call(functools.partial(kernel, cfg), out_shape=(pltpu.VMEM((row...  17.3 us
    pallas_call x1, Pallas kernels, per_device(): pl.pallas_call(finish, out_shape=jax.ShapeDtypeStruct((rows, rhs), BF16),...  1.34 us

profile of v4, /device:TPU:0, one launch (start us, length us, event | category | flops | bytes accessed | tf_op | source)
XLA Modules:
  0.0 18.7 jit_solution(12111897092344027947)
XLA Ops:
  0.0 17.3 %shard_map.64 = (f32[1024,640]{1,0:T(8,128)S(1)}, bf16[1024,160]{1,0:T(8,128)(2,1)S(1)}, bf16[160,640]{1,0:T(8,128)(2,1)S(1)}) custom-call(s32[6]{0:T(128)} %ranks_hbm.1, s32[1,1024]{1,0:T(1,128)} %bitcast.1, bf16[1024,640]{1,0:T(8,128)(2,1)} %src_hbm.1, bf16[1024,512]{1,0:T(8,128)(2,1)} %leaf_hbm.1, bf16[6,32,1024]{2,1,0:T(8,128)(2,1)} %u_hbm.1, ...), custom_call_target="tpu_custom_call" | custom-call | tf_op jit(solution)/shard_map/pallas_call | solution.py:367
  17.3 1.3 %shard_map.65 = bf16[1024,640]{1,0:T(8,128)(2,1)} custom-call(f32[1024,640]{1,0:T(8,128)S(1)} %get-tuple-element.8.acc, bf16[1024,160]{1,0:T(8,128)(2,1)S(1)} %get-tuple-element.9.u_perm, bf16[160,640]{1,0:T(8,128)(2,1)S(1)} %get-tuple-element.10.far), custom_call_target="tpu_custom_call" | custom-call | tf_op jit(solution)/shard_map/pallas_call | solution.py:381
